TPU v7x, 32 devices: a whole 2x2x4 slice. The times are simulated.
32 devices in a mesh: dp: 8 (over z, x), var: 4 (over y, core).
Axes of the slice: x: 2, y: 2, z: 4, core: 2. Of those that a mesh axis runs over, the one named last changes fastest.
Arguments:
- pixels: bfloat16 [8, 24, 4, 256], P('dp', 'var'), may hold values from -6 to 6
- var_ids: int32 [8, 24], P('dp', 'var'), may hold values from 0 to 90, as said below
- counts: int32 [8], P('dp'), may hold values from 3 to 24, as said below
- patch_weight: bfloat16 [91, 4, 1024], replicated, may hold values from -3 to 3
- var_embed: bfloat16 [91, 1024], replicated, may hold values from -5 to 5
- norm_gain: float32 [1024], replicated, may hold values from 0.1 to 1.9
- norm_bias: float32 [1024], replicated, may hold values from -3 to 3
- key_weight: bfloat16 [1024, 1024], P('dp'), may hold values from -0.1875 to 0.1875
- value_weight: bfloat16 [1024, 1024], P('dp'), may hold values from -0.1875 to 0.1875
- query: float32 [16, 64], replicated, may hold values from -200 to 200
- out_weight: bfloat16 [1024, 1024], replicated, may hold values from -0.1875 to 0.1875
Outputs:
- aggregated: bfloat16 [8, 256, 1024], P('dp', 'var')
Inputs may be any that keep to these rules, and one draw needn't show every extreme that they name: `var_ids`: in each sample the ids of slots below its count are distinct; slots at or past the count are padding with arbitrary ids. `counts`: some sample has exactly min(91, 24) live slots and some has exactly 3.
All inputs are finite; a program needn't handle non-finite values.
Results may differ from a plain program's by a relative error of at most 0.018.
Values may be sent and summed in bfloat16 or wider, within the bound.
A program may use at most 64 MiB of HBM per device.

v0:
```python
import math

import jax
import jax.numpy as jnp
from jax import lax
from jax.sharding import PartitionSpec as P


def on_device(
    pixels,
    var_ids,
    counts,
    patch_weight,
    var_embed,
    norm_gain,
    norm_bias,
    key_weight,
    value_weight,
    query,
    out_weight,
):
    slots = pixels.shape[1]
    patches = pixels.shape[3]
    width = out_weight.shape[0]
    heads = query.shape[0]
    head_size = query.shape[1]
    ids = var_ids[0]
    table = patch_weight[ids]
    embedded = jnp.einsum("skp,skd->spd", pixels[0], table, preferred_element_type=jnp.float32)
    embedded = embedded + var_embed[ids].astype(jnp.float32)[:, None, :]
    center = embedded - jnp.mean(embedded, axis=-1, keepdims=True)
    spread = jnp.mean(center * center, axis=-1, keepdims=True)
    normed = (center * lax.rsqrt(spread + 1e-05) * norm_gain + norm_bias).astype(jnp.bfloat16)
    flat = normed.reshape(slots * patches, width)
    local_fold = jnp.einsum(
        "jhe,he->jh",
        key_weight.astype(jnp.float32).reshape(-1, heads, head_size),
        query,
        precision=lax.Precision.HIGHEST,
    )
    folded = lax.all_gather(local_fold, "dp", axis=0, tiled=True)
    values = jnp.dot(
        flat,
        lax.all_gather(value_weight, "dp", axis=0, tiled=True),
        preferred_element_type=jnp.float32,
    )
    scores = jnp.dot(flat.astype(jnp.float32), folded, precision=lax.Precision.HIGHEST)
    scores = (scores * (1.0 / math.sqrt(head_size))).reshape(slots, patches, heads)
    first_slot = lax.axis_index("var") * slots
    live = (first_slot + jnp.arange(slots, dtype=jnp.int32) < counts[0])[:, None, None]
    scores = jnp.where(live, scores, jnp.float32(-1e30))
    values = values.astype(jnp.bfloat16).reshape(slots, patches, width)
    values_all = lax.all_to_all(values, "var", split_axis=1, concat_axis=0, tiled=True)
    scores_all = lax.all_to_all(scores, "var", split_axis=1, concat_axis=0, tiled=True)
    owned = scores_all.shape[1]
    peak = jnp.max(scores_all, axis=0)
    expo = jnp.exp(scores_all - peak)
    total = jnp.sum(expo, axis=0)
    numer = jnp.einsum(
        "sph,sphe->phe",
        expo.astype(jnp.bfloat16),
        values_all.reshape(-1, owned, heads, head_size),
        preferred_element_type=jnp.float32,
    )
    mixed = (numer / total[:, :, None]).reshape(-1, width).astype(jnp.bfloat16)
    return jnp.dot(mixed, out_weight, preferred_element_type=jnp.float32).astype(jnp.bfloat16)[None]


def solution(mesh):
    placed = (
        P("dp", "var", None, None),
        P("dp", "var"),
        P("dp"),
        P(),
        P(),
        P(),
        P(),
        P("dp", None),
        P("dp", None),
        P(),
        P(),
    )
    return jax.shard_map(
        on_device, mesh=mesh, in_specs=placed, out_specs=P("dp", "var", None), check_vma=False
    )
```

profile of v0, /device:TPU:0, one launch (start us, length us, event | category | flops | bytes accessed | tf_op | source)
XLA Modules:
  0.0 155.5 jit_solution(17821916475907785103)
XLA Ops:
  6.5 0.0 copy-start
  6.5 0.0 all-gather.2.cloned.1.call-start
  6.5 0.7 all-gather.2.cloned.1.call-update
  7.3 0.7 fusion.7
  7.9 1.5 gather_fusion.1
  9.5 1.7 %gather_fusion = bf16[6,4,1024]{2,1,0:T(4,128)(2,1)S(1)} fusion(bf16[91,4,1024]{2,1,0:T(4,128)(2,1)} %param.14, s32[1024]{0:T(1024)S(1)} %pad_clamp_fusion), kind=kCustom, calls=%fused_computation | custom fusion | bytes 98328 | tf_op jit(solution)/shard_map/gather | solution.py:28
  11.2 1.1 copy.28
  12.3 1.0 fusion.8
  13.3 32.6 %all_gather.6 = f32[1024,16]{0,1:T(8,128)S(1)} all-gather(f32[128,16]{0,1:T(8,128)S(1)} %bitcast.71), channel_id=1, replica_groups=mesh['dp'=8,'var'=4] {'dp'}, dimensions={0}, use_global_device_ids=true | all-gather | bytes 73728 | tf_op jit(solution)/shard_map/all_gather | solution.py:41
  45.9 0.0 copy-start.2
  46.0 0.0 copy-start.3
  46.0 1.8 %bitcast_reduce_fusion = (f32[6,256]{1,0:T(8,128)S(1)}, f32[6,1024,256]{1,2,0:T(8,128)S(1)}) fusion(f32[6,1024]{1,0:T(8,128)S(1)} %convert_element_type.27, bf16[6,4,1024]{2,1,0:T(4,128)(2,1)S(1)} %gather_fusion, bf16[1,6,4,256]{3,2,1,0:T(4,128)(2,1)} %param.11), kind=kOutput, calls=%fused_computation.3 | convolution fusion | flops 15727104 | bytes 6383616 | tf_op jit(solution)/shard_map/skp,skd->spd/dot_general | solution.py:29
  47.8 1.0 multiply_reduce_fusion
  48.8 0.0 copy-done.2
  48.8 0.0 copy-done.3
  48.8 1.4 add_convert_fusion
  50.2 0.0 copy-start.1
  50.2 1.7 %copy-done.1 = bf16[6,256,1024]{2,1,0:T(8,128)(2,1)} copy-done((bf16[6,256,1024]{2,1,0:T(8,128)(2,1)}, bf16[6,256,1024]{2,1,0:T(8,128)(2,1)S(1)}, u32[]{:S(2)}) %copy-start.1) | copy-done | bytes 3145752
  51.9 2.5 %convolution_multiply_fusion = f32[1536,16]{0,1:T(8,128)S(1)} fusion(bf16[1536,1024]{1,0:T(8,128)(2,1)S(1)} %bitcast.62, f32[1024,16]{0,1:T(8,128)S(1)} %all_gather.6), kind=kOutput, calls=%fused_computation.9 | convolution fusion | flops 302014464 | bytes 3309568 | tf_op jit(solution)/shard_map/dot_general | solution.py:47
  55.2 0.1 broadcast_select_fusion
  55.2 0.4 copy.29
  55.7 1.0 reshape.95
  56.7 3.3 %all-to-all-start = ((f32[4,1,6144]{2,1,0:T(1,128)}), f32[4,1,6144]{2,1,0:T(1,128)S(1)}, u32[]{:S(2)}, u32[]{:S(2)}) async-start(f32[4,1,6144]{2,1,0:T(1,128)} %reshape.95), calls=%async_computation | async-start | bytes 196608 | tf_op jit(solution)/shard_map/all_to_all | solution.py:54
  60.0 1.5 all-gather.2.cloned.1.call-done
  61.5 6.0 %convolution_convert_fusion = bf16[1536,1024]{1,0:T(8,128)(2,1)S(1)} fusion(bf16[1536,1024]{1,0:T(8,128)(2,1)} %bitcast.63, bf16[1024,1024]{1,0:T(8,128)(2,1)} %all-gather.2.cloned.1.call-done), kind=kOutput, calls=%fused_computation.8 | convolution fusion | flops 3222798336 | bytes 8388608 | tf_op jit(solution)/shard_map/dot_general | solution.py:42
  67.5 3.8 %copy.32 = bf16[6,256,1024]{2,0,1:T(8,128)(2,1)} copy(bf16[6,256,1024]{2,1,0:T(8,128)(2,1)S(1)} %bitcast.66) | data formatting | bytes 6291456 | tf_op jit(solution)/shard_map/reshape | solution.py:52
  71.2 0.0 all-to-all-done
  71.2 5.0 %all-to-all-start.1 = ((bf16[6,256,1024]{2,0,1:T(8,128)(2,1)}), bf16[6,256,1024]{2,0,1:T(8,128)(2,1)}, u32[]{:S(2)}, u32[]{:S(2)}) async-start(bf16[6,256,1024]{2,0,1:T(8,128)(2,1)} %copy.32), calls=%async_computation.1 | async-start | bytes 8388608 | tf_op jit(solution)/shard_map/all_to_all | solution.py:53
  76.3 0.5 broadcast.67
  76.8 0.9 reduce.2
  77.7 0.5 reshape.96
  78.2 0.3 copy.41
  78.5 0.1 bitcast_reduce_fusion.1
  78.6 0.5 copy.38
  79.2 0.1 exponential_reduce_fusion
  79.3 0.1 copy.35
  79.4 44.9 %all-to-all-done.1 = bf16[6,256,1024]{2,0,1:T(8,128)(2,1)} async-done(((bf16[6,256,1024]{2,0,1:T(8,128)(2,1)}), bf16[6,256,1024]{2,0,1:T(8,128)(2,1)}, u32[]{:S(2)}, u32[]{:S(2)}) %all-to-all-start.1) | async-done | bytes 3145760 | tf_op jit(solution)/shard_map/all_to_all | solution.py:53
  124.3 5.6 %copy.34 = bf16[4,6,64,1024]{3,2,1,0:T(8,128)(2,1)} copy(bf16[4,6,64,1024]{3,1,2,0:T(8,128)(2,1)} %bitcast.19) | data formatting | bytes 6291456 | tf_op jit(solution)/shard_map/all_to_all | solution.py:53
  129.9 9.2 %reshape.74 = bf16[24,64,16,64]{3,2,1,0:T(8,128)(2,1)} reshape(bf16[4,6,64,1024]{3,2,1,0:T(8,128)(2,1)} %copy.34) | data formatting | bytes 6291456 | tf_op jit(solution)/shard_map/reshape | solution.py:62
  139.1 8.0 %fusion = f32[64,16,1,64]{3,2,1,0:T(1,128)S(1)} fusion(bf16[24,64,16,1]{0,3,2,1:T(2,128)(2,1)S(1)} %copy.38, bf16[24,64,16,64]{3,2,1,0:T(8,128)(2,1)} %reshape.74), kind=kOutput, calls=%fused_computation.4 | convolution fusion | flops 3145728 | bytes 3457024 | tf_op jit(solution)/shard_map/sph,sphe->phe/dot_general | solution.py:59
  147.1 0.2 divide_convert_fusion
  147.3 0.2 convert_element_type.32
  147.5 0.0 copy-done
  147.5 1.1 fusion.2
  (8 shorter events, 0.1 us)
Async XLA Ops:
  6.5 141.0 %copy-start = (bf16[1024,1024]{1,0:T(8,128)(2,1)S(1)}, bf16[1024,1024]{1,0:T(8,128)(2,1)}, u32[]{:S(2)}) copy-start(bf16[1024,1024]{1,0:T(8,128)(2,1)} %param.21) | copy-start | bytes 6291460
  6.5 54.9 %all-gather.2.cloned.1.call-start = ((), (), s32[]{:S(2)}) async-start(), calls=%async_computation.2 | async-start | bytes 2359296 | tf_op jit(solution)/shard_map/all_gather | solution.py:44
  45.9 2.9 %copy-start.2 = (f32[1024]{0:T(1024)S(1)}, f32[1024]{0:T(1024)}, u32[]{:S(2)}) copy-start(f32[1024]{0:T(1024)} %param.17) | copy-start | bytes 12292
  46.0 2.9 %copy-start.3 = (f32[1024]{0:T(1024)S(1)}, f32[1024]{0:T(1024)}, u32[]{:S(2)}) copy-start(f32[1024]{0:T(1024)} %param.16) | copy-start | bytes 12292
  50.2 1.7 %copy-start.1 = (bf16[6,256,1024]{2,1,0:T(8,128)(2,1)}, bf16[6,256,1024]{2,1,0:T(8,128)(2,1)S(1)}, u32[]{:S(2)}) copy-start(bf16[6,256,1024]{2,1,0:T(8,128)(2,1)S(1)} %add_convert_fusion) | copy-start | bytes 9437188
  56.7 14.5 %all-to-all-start = ((f32[4,1,6144]{2,1,0:T(1,128)}), f32[4,1,6144]{2,1,0:T(1,128)S(1)}, u32[]{:S(2)}, u32[]{:S(2)}) async-start(f32[4,1,6144]{2,1,0:T(1,128)} %reshape.95), calls=%async_computation | async-start | bytes 196608 | tf_op jit(solution)/shard_map/all_to_all | solution.py:54
  71.2 53.1 %all-to-all-start.1 = ((bf16[6,256,1024]{2,0,1:T(8,128)(2,1)}), bf16[6,256,1024]{2,0,1:T(8,128)(2,1)}, u32[]{:S(2)}, u32[]{:S(2)}) async-start(bf16[6,256,1024]{2,0,1:T(8,128)(2,1)} %copy.32), calls=%async_computation.1 | async-start | bytes 8388608 | tf_op jit(solution)/shard_map/all_to_all | solution.py:53
Sparse Core Ops, SparseCore 0:
  9.5 51.9 all-gather.1
where the time goes:
time: 156 us; the launch traced here: 155 us
  waiting for transfers between devices  47.1 us (30%)
  blocking collectives  32.6 us (21%)
  local copies, waits for them, and re-layouts  28.3 us (18%)
  matrix products  20.4 us (13%)
  between operations  14.2 us (9%)
  starting transfers between devices  8.35 us (5%)
  other arithmetic  4.48 us (3%)
    all_to_all x1, waiting for transfers between devices, on_device(): lax.all_to_all(values, 'var', split_axis=1, concat_axis=0, tiled=True)  44.9 us
    all_gather x1, blocking collectives, on_device(): folded = lax.all_gather(local_fold, 'dp', axis=0, tiled=True)  32.6 us
    reshape x1, local copies, waits for them, and re-layouts, on_device(): values_all.reshape(-1, owned, heads, head_size)  9.19 us
    dot_general x1, matrix products, on_device(): jnp.einsum('sph,sphe->phe', expo.astype(jnp.bfloat16), values_all.reshape...  7.95 us
    dot_general x1, matrix products, on_device(): jnp.dot(flat, lax.all_gather(value_weight, 'dp', axis=0, tiled=True), pre...  5.98 us
    all_to_all x1, local copies, waits for them, and re-layouts, on_device(): lax.all_to_all(values, 'var', split_axis=1, concat_axis=0, tiled=True)  5.62 us
    all_to_all x1, starting transfers between devices, on_device(): lax.all_to_all(values, 'var', split_axis=1, concat_axis=0, tiled=True)  5.04 us
    unnamed x11, local copies, waits for them, and re-layouts  4.28 us
  transfers between devices with their start and end apart: 3, of which 2 were waited for; matrix products, arithmetic and copies ran while one was open for 17% of the time, Pallas kernels for 0%

commit v1 on v0

v1 whole, which is shorter than its diff:
```python
import functools
import math

import jax
import jax.numpy as jnp
from jax import lax
from jax.experimental import pallas as pl
from jax.experimental.pallas import tpu as pltpu
from jax.sharding import PartitionSpec as P

F32 = jnp.float32
BF16 = jnp.bfloat16
EXACT = lax.Precision.HIGHEST


def rounded_up(value, unit):
    return -(-value // unit) * unit


def kernel(
    dims,
    ids_ref,
    counts_ref,
    pixels_ref,
    table_hbm,
    embed_hbm,
    gain_ref,
    bias_ref,
    key_hbm,
    value_hbm,
    query_ref,
    out_hbm,
    result_ref,
    table,
    embed,
    key_block,
    wout,
    value_all,
    fold_all,
    rows_f32,
    rows_all,
    coeff_all,
    basis,
    mix_send,
    mix_recv,
    local_sem,
    value_ss,
    value_rs,
    fold_ss,
    fold_rs,
    rows_ss,
    rows_rs,
    coeff_ss,
    coeff_rs,
    mix_ss,
    mix_rs,
):
    n, nv, groups, slots, taps, patches, width, heads, head_size = dims
    padded = rows_f32.shape[1]
    depth = key_block.shape[0]
    columns = key_block.shape[1]
    local_heads = heads // groups
    half = patches * groups // nv
    owned = patches // nv
    basis_rows = nv * (taps + 2) * padded

    b = lax.axis_index("dp")
    v = lax.axis_index("var")
    r, g = v // groups, v % groups
    pair = n % 2 == 0
    lo_size = 2 if pair else 1
    hi_size = n // lo_size
    hi, lo = b // lo_size, b % lo_size

    def remote(src, dst, ss, rs, **where):
        return pltpu.make_async_remote_copy(
            src_ref=src,
            dst_ref=dst,
            send_sem=ss,
            recv_sem=rs,
            device_id=where,
            device_id_type=pl.DeviceIdType.MESH,
        )

    barrier = pltpu.get_barrier_semaphore()
    for off in range(1, n):
        pl.semaphore_signal(
            barrier, inc=1, device_id={"dp": (b + off) % n}, device_id_type=pl.DeviceIdType.MESH
        )
    for off in range(1, nv):
        pl.semaphore_signal(
            barrier, inc=1, device_id={"var": (v + off) % nv}, device_id_type=pl.DeviceIdType.MESH
        )

    mine = pl.ds(pl.multiple_of(g * columns, columns), columns)
    get_key = pltpu.make_async_copy(key_hbm.at[:, mine], key_block, local_sem.at[0])
    get_value = pltpu.make_async_copy(value_hbm.at[:, mine], value_all.at[b], local_sem.at[1])
    get_table = pltpu.make_async_copy(table_hbm, table, local_sem.at[2])
    get_embed = pltpu.make_async_copy(embed_hbm, embed, local_sem.at[3])
    get_out = pltpu.make_async_copy(out_hbm, wout, local_sem.at[4])
    get_value.start()
    get_key.start()
    get_table.start()
    get_embed.start()
    get_out.start()

    fold_rows = fold_all.shape[1]
    pick = (
        lax.broadcasted_iota(jnp.int32, (fold_rows, heads), 1)
        == lax.broadcasted_iota(jnp.int32, (fold_rows, heads), 0) + g * local_heads
    ).astype(F32)
    own_query = jnp.dot(pick, query_ref[...], precision=EXACT, preferred_element_type=F32)
    spread_out = (
        lax.broadcasted_iota(jnp.int32, (head_size, columns), 1) % head_size
        == lax.broadcasted_iota(jnp.int32, (head_size, columns), 0)
    ).astype(F32)
    tiled = jnp.dot(own_query, spread_out, precision=EXACT, preferred_element_type=F32)
    own_head = (
        lax.broadcasted_iota(jnp.int32, (fold_rows, columns), 1) // head_size
        == lax.broadcasted_iota(jnp.int32, (fold_rows, columns), 0)
    )
    diagonal = jnp.where(own_head, tiled, 0.0) * (1.0 / math.sqrt(head_size))

    get_value.wait()
    pl.semaphore_wait(barrier, n + nv - 2)

    value_sends = []

    def send_value(owner, sem, **where):
        copy = remote(
            value_all.at[owner], value_all.at[owner], value_ss.at[sem], value_rs.at[sem], **where
        )
        copy.start()
        value_sends.append(copy)

    def value_from(owner, sem):
        return remote(
            value_all.at[owner], value_all.at[owner], value_ss.at[sem], value_rs.at[sem], dp=b
        )

    mate = hi * lo_size + (lo_size - 1 - lo)
    if pair:
        send_value(b, hi_size, dp=mate)
    for off in range(1, hi_size):
        send_value(b, off, dp=((hi + off) % hi_size) * lo_size + lo)

    get_key.wait()
    fold_all[b] = lax.dot_general(
        diagonal,
        key_block[...].astype(F32),
        (((1,), (1,)), ((), ())),
        precision=EXACT,
        preferred_element_type=F32,
    )

    rows_f32[...] = jnp.zeros_like(rows_f32)
    get_table.wait()
    get_embed.wait()
    slot_of = lax.broadcasted_iota(jnp.int32, (padded, embed.shape[0]), 0)
    wanted = jnp.full((padded, embed.shape[0]), -1, jnp.int32)
    for s in range(slots):
        rows = table[ids_ref[0, s]].astype(F32)
        for k in range(taps):
            rows_f32[k, s : s + 1, :] = rows[k : k + 1, :]
        wanted = jnp.where(slot_of == s, ids_ref[0, s], wanted)
    hot = (wanted == lax.broadcasted_iota(jnp.int32, wanted.shape, 1)).astype(BF16)
    rows_f32[taps] = jnp.dot(hot, embed[...], preferred_element_type=F32)
    rows_all[v] = rows_f32[...].astype(BF16)

    fold_sends = []
    for off in range(1, n):
        copy = remote(
            fold_all.at[b], fold_all.at[b], fold_ss.at[off], fold_rs.at[off], dp=(b + off) % n
        )
        copy.start()
        fold_sends.append(copy)

    centred = []
    for k in range(taps + 1):
        row = rows_f32[k]
        centred.append(row - jnp.mean(row, axis=-1, keepdims=True))

    rows_sends = []
    for off in range(1, nv):
        copy = remote(
            rows_all.at[v], rows_all.at[v], rows_ss.at[off], rows_rs.at[off], var=(v + off) % nv
        )
        copy.start()
        rows_sends.append(copy)

    pix = pixels_ref[0].astype(F32)
    fill = jnp.zeros((padded - slots, patches), F32)
    field = []
    for k in range(taps):
        own = [pix[s, k : k + 1, :] for s in range(slots)]
        field.append(jnp.concatenate(own + ([fill] if padded > slots else []), axis=0))
    field.append(jnp.ones((padded, patches), F32))
    variance = jnp.zeros((padded, patches), F32)
    for k in range(taps + 1):
        for m in range(k, taps + 1):
            gram = jnp.mean(centred[k] * centred[m], axis=-1, keepdims=True)
            variance += (1.0 if m == k else 2.0) * gram * (field[k] * field[m])
    scale = lax.rsqrt(jnp.maximum(variance, 0.0) + 1e-05)
    for k in range(taps + 1):
        coeff_all[v, k] = field[k] * scale

    def forward(off):
        owner = ((hi + hi_size - off) % hi_size) * lo_size + lo
        value_from(owner, off).wait_recv()
        if pair:
            send_value(owner, hi_size + off, dp=mate)

    if hi_size > 1:
        forward(1)
    coeff_sends = []
    for off in range(1, nv):
        copy = remote(
            coeff_all.at[v], coeff_all.at[v], coeff_ss.at[off], coeff_rs.at[off], var=(v + off) % nv
        )
        copy.start()
        coeff_sends.append(copy)
    for off in range(2, hi_size):
        forward(off)

    gain = gain_ref[...]
    for off in range(nv):
        src = (v + nv - off) % nv
        if off:
            remote(
                rows_all.at[src], rows_all.at[src], rows_ss.at[off], rows_rs.at[off], var=v
            ).wait_recv()
        for k in range(taps + 1):
            row = rows_all[src, k].astype(F32)
            basis[src, k] = (row - jnp.mean(row, axis=-1, keepdims=True)) * gain
        basis[src, taps + 1] = jnp.broadcast_to(bias_ref[...], (padded, width))

    for off in range(1, n):
        src = (b + n - off) % n
        remote(
            fold_all.at[src], fold_all.at[src], fold_ss.at[off], fold_rs.at[off], dp=b
        ).wait_recv()
    flat = basis[...].reshape(basis_rows, width)
    folded = jnp.concatenate([fold_all[i] for i in range(n)], axis=1)
    score_of = lax.dot_general(
        flat, folded, (((1,), (1,)), ((), ())), precision=EXACT, preferred_element_type=F32
    ).reshape(nv, taps + 2, padded, fold_rows)

    for off in range(1, nv):
        src = (v + nv - off) % nv
        remote(
            coeff_all.at[src], coeff_all.at[src], coeff_ss.at[off], coeff_rs.at[off], var=v
        ).wait_recv()
    window = pl.ds(pl.multiple_of(r * half, half), half)
    coeff = [coeff_all[:, k, :, window] for k in range(taps + 1)]
    place = lax.broadcasted_iota(jnp.int32, (nv, padded, half), 1)
    slot = lax.broadcasted_iota(jnp.int32, (nv, padded, half), 0) * slots + place
    live = (place < slots) & (slot < counts_ref[0])
    weights = []
    for h in range(local_heads):
        score = jnp.broadcast_to(score_of[:, taps + 1, :, h : h + 1], (nv, padded, half))
        for k in range(taps + 1):
            score = score + coeff[k] * score_of[:, k, :, h : h + 1]
        score = jnp.where(live, score, -1e30)
        peak = jnp.max(jnp.max(score, axis=0, keepdims=True), axis=1, keepdims=True)
        expo = jnp.exp(score - peak)
        total = jnp.sum(jnp.sum(expo, axis=0, keepdims=True), axis=1, keepdims=True)
        prob = expo / total
        parts = [prob * coeff[k] for k in range(taps + 1)] + [prob]
        weights.append(jnp.stack(parts, axis=1).reshape(basis_rows, half).astype(BF16))

    if pair:
        for off in range(hi_size):
            owner = ((hi + hi_size - off) % hi_size) * lo_size + (lo_size - 1 - lo)
            value_from(owner, hi_size + off).wait_recv()
    projected = jnp.dot(
        flat.astype(BF16),
        value_all[...].reshape(width, columns),
        preferred_element_type=F32,
    ).astype(BF16)
    mixed = jnp.concatenate(
        [
            lax.dot_general(
                weights[h],
                projected[:, h * head_size : (h + 1) * head_size],
                (((0,), (0,)), ((), ())),
                preferred_element_type=F32,
            )
            for h in range(local_heads)
        ],
        axis=1,
    ).astype(BF16)
    mix_send[...] = mixed.reshape(groups, owned, columns)

    mix_sends = []
    for off in range(1, groups):
        to = (g + off) % groups
        copy = remote(
            mix_send.at[to], mix_recv.at[g], mix_ss.at[off], mix_rs.at[off], var=r * groups + to
        )
        copy.start()
        mix_sends.append(copy)

    get_out.wait()
    total = jnp.dot(mix_send[g], wout[mine, :], preferred_element_type=F32)
    for off in range(1, groups):
        src = (g + groups - off) % groups
        remote(
            mix_send.at[src], mix_recv.at[src], mix_ss.at[off], mix_rs.at[off], var=v
        ).wait_recv()
        there = pl.ds(pl.multiple_of(src * columns, columns), columns)
        total += jnp.dot(mix_recv[src], wout[there, :], preferred_element_type=F32)
    result_ref[0] = total.astype(result_ref.dtype)

    for copy in value_sends + fold_sends + rows_sends + coeff_sends + mix_sends:
        copy.wait_send()


def on_device(
    n,
    nv,
    pixels,
    var_ids,
    counts,
    patch_weight,
    var_embed,
    norm_gain,
    norm_bias,
    key_weight,
    value_weight,
    query,
    out_weight,
):
    slots, taps, patches = pixels.shape[1:]
    width = out_weight.shape[0]
    heads, head_size = query.shape
    groups = min(nv, width // 128)
    columns = width // groups
    depth = value_weight.shape[0]
    padded = rounded_up(slots, 8)
    owned = patches // nv
    fold_rows = rounded_up(heads // groups, 8)
    vmem = pl.BlockSpec(memory_space=pltpu.VMEM)
    smem = pl.BlockSpec(memory_space=pltpu.SMEM)
    hbm = pl.BlockSpec(memory_space=pl.ANY)
    dims = (n, nv, groups, slots, taps, patches, width, heads, head_size)
    dma = pltpu.SemaphoreType.DMA
    return pl.pallas_call(
        functools.partial(kernel, dims),
        out_shape=jax.ShapeDtypeStruct((1, owned, width), BF16),
        in_specs=[smem, smem, vmem, hbm, hbm, vmem, vmem, hbm, hbm, vmem, hbm],
        out_specs=vmem,
        scratch_shapes=[
            pltpu.VMEM(patch_weight.shape, BF16),
            pltpu.VMEM(var_embed.shape, BF16),
            pltpu.VMEM((depth, columns), BF16),
            pltpu.VMEM((width, width), BF16),
            pltpu.VMEM((n, depth, columns), BF16),
            pltpu.VMEM((n, fold_rows, depth), F32),
            pltpu.VMEM((taps + 1, padded, width), F32),
            pltpu.VMEM((nv, taps + 1, padded, width), BF16),
            pltpu.VMEM((nv, taps + 1, padded, patches), F32),
            pltpu.VMEM((nv, taps + 2, padded, width), F32),
            pltpu.VMEM((groups, owned, columns), BF16),
            pltpu.VMEM((groups, owned, columns), BF16),
            dma((5,)),
            dma((n,)),
            dma((n,)),
            dma((n,)),
            dma((n,)),
            dma((nv,)),
            dma((nv,)),
            dma((nv,)),
            dma((nv,)),
            dma((groups,)),
            dma((groups,)),
        ],
        compiler_params=pltpu.CompilerParams(collective_id=0, has_side_effects=True),
    )(
        var_ids,
        counts,
        pixels,
        patch_weight,
        var_embed,
        norm_gain.reshape(1, width),
        norm_bias.reshape(1, width),
        key_weight,
        value_weight,
        query,
        out_weight,
    )


def solution(mesh):
    placed = (
        P("dp", "var", None, None),
        P("dp", "var"),
        P("dp"),
        P(),
        P(),
        P(),
        P(),
        P("dp", None),
        P("dp", None),
        P(),
        P(),
    )
    return jax.shard_map(
        functools.partial(on_device, mesh.shape["dp"], mesh.shape["var"]),
        mesh=mesh,
        in_specs=placed,
        out_specs=P("dp", "var", None),
        check_vma=False,
    )
```

time: 156 us -> 24.8 us (0.16)
  waiting for transfers between devices: 47.1 us -> 0 us
  blocking collectives: 32.6 us -> 0 us
  local copies, waits for them, and re-layouts: 28.3 us -> 1.57 us
  Pallas kernels: 0 us -> 22.4 us
  matrix products: 20.4 us -> 0 us
  between operations: 14.2 us -> 0.66 us
  starting transfers between devices: 8.35 us -> 0 us
  other arithmetic: 4.48 us -> 0 us
    all_to_all x2 -> x0, waiting for transfers between devices: 44.9 us -> none  [the longest x1 44.9 us: on_device(): lax.all_to_all(values, 'var', split_axis=1, concat_axis=0, tiled=True)]
    all_gather x1 -> x0, blocking collectives: 32.6 us -> none  [on_device(): folded = lax.all_gather(local_fold, 'dp', axis=0, tiled=True)]
    pallas_call x0 -> x1, Pallas kernels: none -> 22.4 us  [on_device(): pl.pallas_call(functools.partial(kernel, dims), out_shape=jax.ShapeDtypeS...]
    dot_general x6 -> x0, matrix products: 20.4 us -> none  [the longest x1 7.95 us: on_device(): jnp.einsum('sph,sphe->phe', expo.astype(jnp.bfloat16), values_all.reshape...]
    reshape x3 -> x0, local copies, waits for them, and re-layouts: 13 us -> none  [the longest x1 9.19 us: on_device(): values_all.reshape(-1, owned, heads, head_size)]
    all_to_all x2 -> x0, starting transfers between devices: 8.34 us -> none  [the longest x1 5.04 us: on_device(): lax.all_to_all(values, 'var', split_axis=1, concat_axis=0, tiled=True)]
    all_to_all x4 -> x0, local copies, waits for them, and re-layouts: 6.47 us -> none  [the longest x1 5.62 us: on_device(): lax.all_to_all(values, 'var', split_axis=1, concat_axis=0, tiled=True)]
    gather x2 -> x0, local copies, waits for them, and re-layouts: 3.24 us -> none  [the longest x1 1.72 us: on_device(): table = patch_weight[ids]]
  transfers between devices with their start and end apart: 3 -> 0, of which waited for: 2 -> 0; matrix products, arithmetic and copies ran while one was open for 17% -> 0% of each run, Pallas kernels for 0% -> 0%
where the time goes in v1:
time: 24.8 us; the launch traced here: 24.6 us
  Pallas kernels  22.4 us (90%)
  local copies, waits for them, and re-layouts  1.57 us (6%)
  between operations  0.66 us (3%)
    pallas_call x1, Pallas kernels, on_device(): pl.pallas_call(functools.partial(kernel, dims), out_shape=jax.ShapeDtypeS...  22.4 us
    unnamed x1, local copies, waits for them, and re-layouts  1.57 us

profile of v1, /device:TPU:0, one launch (start us, length us, event | category | flops | bytes accessed | tf_op | source)
XLA Modules:
  0.0 24.6 jit_solution(9116692624541389698)
XLA Ops:
  0.7 22.4 %shard_map.109 = bf16[1,64,1024]{2,1,0:T(8,128)(2,1)} custom-call(s32[1,6]{1,0:T(1,128)} %ids_ref.1, s32[1]{0:T(128)S(6)} %copy.13.counts_ref, bf16[1,6,4,256]{3,2,1,0:T(4,128)(2,1)} %pixels_ref.1, bf16[91,4,1024]{2,1,0:T(4,128)(2,1)} %table_hbm.1, bf16[91,1024]{1,0:T(8,128)(2,1)} %embed_hbm.1, f32[1,1024]{1,0:T(1,128)} %bitcast.2, f32[1,1024]{1,0:T(1,128)} %bitcast.3, ...), custom_call_target="tpu_custom_call" | custom-call | tf_op jit(solution)/shard_map/pallas_call | solution.py:347
  23.1 1.6 %copy.14 = bf16[1,64,1024]{2,1,0:T(8,128)(2,1)} copy(bf16[1,64,1024]{2,1,0:T(8,128)(2,1)} %shard_map.109) | data formatting | bytes 262144

commit v2 on v1

--- a/solution.py
+++ b/solution.py
@@ -38,7 +38,7 @@
     value_all,
     fold_all,
     rows_f32,
-    rows_all,
+    ids_all,
     coeff_all,
     basis,
     mix_send,
@@ -48,8 +48,8 @@
     value_rs,
     fold_ss,
     fold_rs,
-    rows_ss,
-    rows_rs,
+    ids_ss,
+    ids_rs,
     coeff_ss,
     coeff_rs,
     mix_ss,
@@ -58,6 +58,7 @@
     n, nv, groups, slots, taps, patches, width, heads, head_size = dims
     padded = rows_f32.shape[1]
     depth = key_block.shape[0]
+    parts = value_ss.shape[0] // n
     columns = key_block.shape[1]
     local_heads = heads // groups
     half = patches * groups // nv
@@ -67,10 +68,11 @@
     b = lax.axis_index("dp")
     v = lax.axis_index("var")
     r, g = v // groups, v % groups
-    pair = n % 2 == 0
-    lo_size = 2 if pair else 1
-    hi_size = n // lo_size
-    hi, lo = b // lo_size, b % lo_size
+    def ahead(mask):
+        return (b // 2 + mask // 2) % (n // 2) * 2 + (b % 2 + mask) % 2
+
+    def across(mask):
+        return (b // 2 + n // 2 - mask // 2) % (n // 2) * 2 + (b % 2 + mask) % 2
 
     def remote(src, dst, ss, rs, **where):
         return pltpu.make_async_remote_copy(
@@ -82,10 +84,15 @@
             device_id_type=pl.DeviceIdType.MESH,
         )
 
+    def onward(mask):
+        if mask == 0:
+            return [1] * (n > 1) + [m for m in range(2, n, 2)]
+        return [1] * (mask % 2 == 0)
+
     barrier = pltpu.get_barrier_semaphore()
-    for off in range(1, n):
+    for bit in onward(0):
         pl.semaphore_signal(
-            barrier, inc=1, device_id={"dp": (b + off) % n}, device_id_type=pl.DeviceIdType.MESH
+            barrier, inc=1, device_id={"dp": ahead(bit)}, device_id_type=pl.DeviceIdType.MESH
         )
     for off in range(1, nv):
         pl.semaphore_signal(
@@ -102,7 +109,6 @@
     get_key.start()
     get_table.start()
     get_embed.start()
-    get_out.start()
 
     fold_rows = fold_all.shape[1]
     pick = (
@@ -121,29 +127,6 @@
     )
     diagonal = jnp.where(own_head, tiled, 0.0) * (1.0 / math.sqrt(head_size))
 
-    get_value.wait()
-    pl.semaphore_wait(barrier, n + nv - 2)
-
-    value_sends = []
-
-    def send_value(owner, sem, **where):
-        copy = remote(
-            value_all.at[owner], value_all.at[owner], value_ss.at[sem], value_rs.at[sem], **where
-        )
-        copy.start()
-        value_sends.append(copy)
-
-    def value_from(owner, sem):
-        return remote(
-            value_all.at[owner], value_all.at[owner], value_ss.at[sem], value_rs.at[sem], dp=b
-        )
-
-    mate = hi * lo_size + (lo_size - 1 - lo)
-    if pair:
-        send_value(b, hi_size, dp=mate)
-    for off in range(1, hi_size):
-        send_value(b, off, dp=((hi + off) % hi_size) * lo_size + lo)
-
     get_key.wait()
     fold_all[b] = lax.dot_general(
         diagonal,
@@ -153,41 +136,27 @@
         preferred_element_type=F32,
     )
 
-    rows_f32[...] = jnp.zeros_like(rows_f32)
     get_table.wait()
     get_embed.wait()
+    get_out.start()
     slot_of = lax.broadcasted_iota(jnp.int32, (padded, embed.shape[0]), 0)
-    wanted = jnp.full((padded, embed.shape[0]), -1, jnp.int32)
-    for s in range(slots):
-        rows = table[ids_ref[0, s]].astype(F32)
-        for k in range(taps):
-            rows_f32[k, s : s + 1, :] = rows[k : k + 1, :]
-        wanted = jnp.where(slot_of == s, ids_ref[0, s], wanted)
-    hot = (wanted == lax.broadcasted_iota(jnp.int32, wanted.shape, 1)).astype(BF16)
-    rows_f32[taps] = jnp.dot(hot, embed[...], preferred_element_type=F32)
-    rows_all[v] = rows_f32[...].astype(BF16)
-
-    fold_sends = []
-    for off in range(1, n):
-        copy = remote(
-            fold_all.at[b], fold_all.at[b], fold_ss.at[off], fold_rs.at[off], dp=(b + off) % n
-        )
-        copy.start()
-        fold_sends.append(copy)
-
-    centred = []
-    for k in range(taps + 1):
-        row = rows_f32[k]
-        centred.append(row - jnp.mean(row, axis=-1, keepdims=True))
-
-    rows_sends = []
-    for off in range(1, nv):
-        copy = remote(
-            rows_all.at[v], rows_all.at[v], rows_ss.at[off], rows_rs.at[off], var=(v + off) % nv
-        )
-        copy.start()
-        rows_sends.append(copy)
-
+    entry = lax.broadcasted_iota(jnp.int32, (padded, embed.shape[0]), 1)
+
+    def centred_rows(ids):
+        wanted = jnp.full(slot_of.shape, -1, jnp.int32)
+        for s in range(slots):
+            rows = table[ids[s]].astype(F32)
+            for k in range(taps):
+                rows_f32[k, s : s + 1, :] = rows[k : k + 1, :]
+            wanted = jnp.where(slot_of == s, ids[s], wanted)
+        hot = (wanted == entry).astype(BF16)
+        kept = [rows_f32[k] for k in range(taps)]
+        kept.append(jnp.dot(hot, embed[...], preferred_element_type=F32))
+        return [row - jnp.mean(row, axis=-1, keepdims=True) for row in kept]
+
+    rows_f32[...] = jnp.zeros_like(rows_f32)
+
+    centred = centred_rows([ids_ref[0, s] for s in range(slots)])
     pix = pixels_ref[0].astype(F32)
     fill = jnp.zeros((padded - slots, patches), F32)
     field = []
@@ -204,14 +173,48 @@
     for k in range(taps + 1):
         coeff_all[v, k] = field[k] * scale
 
-    def forward(off):
-        owner = ((hi + hi_size - off) % hi_size) * lo_size + lo
-        value_from(owner, off).wait_recv()
-        if pair:
-            send_value(owner, hi_size + off, dp=mate)
-
-    if hi_size > 1:
-        forward(1)
+    get_value.wait()
+    pl.semaphore_wait(barrier, len(onward(0)) + nv - 1)
+
+    cube_sends = []
+
+    def value_copy(mask, part, owner, to):
+        piece = value_all.at[owner, pl.ds(part * (depth // parts), depth // parts)]
+        sem = mask * parts + part
+        return remote(piece, piece, value_ss.at[sem], value_rs.at[sem], dp=to)
+
+    def fold_copy(mask, owner, to):
+        piece = fold_all.at[owner]
+        return remote(piece, piece, fold_ss.at[mask], fold_rs.at[mask], dp=to)
+
+    def spread(make, mask):
+        for bit in onward(mask):
+            copy = make(mask | bit, across(mask), ahead(bit))
+            copy.start()
+            cube_sends.append(copy)
+
+    def take_value(mask):
+        for part in range(parts):
+            value_copy(mask, part, across(mask), b).wait_recv()
+            spread(lambda mask, owner, to: value_copy(mask, part, owner, to), mask)
+
+    def take_fold(mask):
+        fold_copy(mask, across(mask), b).wait_recv()
+        spread(fold_copy, mask)
+
+    relayed = sorted((m for m in range(1, n) if onward(m)), key=lambda m: (bin(m).count("1"), m))
+    last = [m for m in range(1, n) if not onward(m)]
+
+    spread(fold_copy, 0)
+    for part in range(parts):
+        spread(lambda mask, owner, to: value_copy(mask, part, owner, to), 0)
+
+    ids_sends = []
+    for off in range(1, nv):
+        copy = remote(ids_ref, ids_all.at[v], ids_ss.at[off], ids_rs.at[off], var=(v + off) % nv)
+        copy.start()
+        ids_sends.append(copy)
+
     coeff_sends = []
     for off in range(1, nv):
         copy = remote(
@@ -219,26 +222,23 @@
         )
         copy.start()
         coeff_sends.append(copy)
-    for off in range(2, hi_size):
-        forward(off)
 
     gain = gain_ref[...]
     for off in range(nv):
         src = (v + nv - off) % nv
         if off:
-            remote(
-                rows_all.at[src], rows_all.at[src], rows_ss.at[off], rows_rs.at[off], var=v
-            ).wait_recv()
+            remote(ids_ref, ids_all.at[src], ids_ss.at[off], ids_rs.at[off], var=v).wait_recv()
+            centred = centred_rows([ids_all[src, 0, s] for s in range(slots)])
         for k in range(taps + 1):
-            row = rows_all[src, k].astype(F32)
-            basis[src, k] = (row - jnp.mean(row, axis=-1, keepdims=True)) * gain
+            basis[src, k] = centred[k] * gain
         basis[src, taps + 1] = jnp.broadcast_to(bias_ref[...], (padded, width))
 
-    for off in range(1, n):
-        src = (b + n - off) % n
-        remote(
-            fold_all.at[src], fold_all.at[src], fold_ss.at[off], fold_rs.at[off], dp=b
-        ).wait_recv()
+    for mask in relayed:
+        take_fold(mask)
+    for mask in relayed:
+        take_value(mask)
+    for mask in last:
+        take_fold(mask)
     flat = basis[...].reshape(basis_rows, width)
     folded = jnp.concatenate([fold_all[i] for i in range(n)], axis=1)
     score_of = lax.dot_general(
@@ -265,13 +265,11 @@
         expo = jnp.exp(score - peak)
         total = jnp.sum(jnp.sum(expo, axis=0, keepdims=True), axis=1, keepdims=True)
         prob = expo / total
-        parts = [prob * coeff[k] for k in range(taps + 1)] + [prob]
-        weights.append(jnp.stack(parts, axis=1).reshape(basis_rows, half).astype(BF16))
-
-    if pair:
-        for off in range(hi_size):
-            owner = ((hi + hi_size - off) % hi_size) * lo_size + (lo_size - 1 - lo)
-            value_from(owner, hi_size + off).wait_recv()
+        terms = [prob * coeff[k] for k in range(taps + 1)] + [prob]
+        weights.append(jnp.stack(terms, axis=1).reshape(basis_rows, half).astype(BF16))
+
+    for mask in last:
+        take_value(mask)
     projected = jnp.dot(
         flat.astype(BF16),
         value_all[...].reshape(width, columns),
@@ -311,7 +309,7 @@
         total += jnp.dot(mix_recv[src], wout[there, :], preferred_element_type=F32)
     result_ref[0] = total.astype(result_ref.dtype)
 
-    for copy in value_sends + fold_sends + rows_sends + coeff_sends + mix_sends:
+    for copy in cube_sends + ids_sends + coeff_sends + mix_sends:
         copy.wait_send()
 
 
@@ -344,6 +342,7 @@
     hbm = pl.BlockSpec(memory_space=pl.ANY)
     dims = (n, nv, groups, slots, taps, patches, width, heads, head_size)
     dma = pltpu.SemaphoreType.DMA
+    parts = 1
     return pl.pallas_call(
         functools.partial(kernel, dims),
         out_shape=jax.ShapeDtypeStruct((1, owned, width), BF16),
@@ -356,15 +355,15 @@
             pltpu.VMEM((width, width), BF16),
             pltpu.VMEM((n, depth, columns), BF16),
             pltpu.VMEM((n, fold_rows, depth), F32),
-            pltpu.VMEM((taps + 1, padded, width), F32),
-            pltpu.VMEM((nv, taps + 1, padded, width), BF16),
+            pltpu.VMEM((taps, padded, width), F32),
+            pltpu.SMEM((nv, 1, slots), jnp.int32),
             pltpu.VMEM((nv, taps + 1, padded, patches), F32),
             pltpu.VMEM((nv, taps + 2, padded, width), F32),
             pltpu.VMEM((groups, owned, columns), BF16),
             pltpu.VMEM((groups, owned, columns), BF16),
             dma((5,)),
-            dma((n,)),
-            dma((n,)),
+            dma((n * parts,)),
+            dma((n * parts,)),
             dma((n,)),
             dma((n,)),
             dma((nv,)),

time: 24.8 us -> 25.3 us (1.020)
  Pallas kernels: 22.4 us -> 22.9 us
    pallas_call x1, Pallas kernels: 22.4 us -> 22.9 us  [on_device(): pl.pallas_call(functools.partial(kernel, dims), out_shape=jax.ShapeDtypeS...]
where the time goes in v2:
time: 25.3 us; the launch traced here: 25.1 us
  Pallas kernels  22.9 us (91%)
  local copies, waits for them, and re-layouts  1.57 us (6%)
  between operations  0.66 us (3%)
    pallas_call x1, Pallas kernels, on_device(): pl.pallas_call(functools.partial(kernel, dims), out_shape=jax.ShapeDtypeS...  22.9 us
    unnamed x1, local copies, waits for them, and re-layouts  1.57 us

profile of v2, /device:TPU:0, one launch (start us, length us, event | category | flops | bytes accessed | tf_op | source)
XLA Modules:
  0.0 25.1 jit_solution(6442225699182034140)
XLA Ops:
  0.7 22.9 %shard_map.109 = bf16[1,64,1024]{2,1,0:T(8,128)(2,1)} custom-call(s32[1,6]{1,0:T(1,128)} %ids_ref.1, s32[1]{0:T(128)S(6)} %copy.13.counts_ref, bf16[1,6,4,256]{3,2,1,0:T(4,128)(2,1)} %pixels_ref.1, bf16[91,4,1024]{2,1,0:T(4,128)(2,1)} %table_hbm.1, bf16[91,1024]{1,0:T(8,128)(2,1)} %embed_hbm.1, f32[1,1024]{1,0:T(1,128)} %bitcast.2, f32[1,1024]{1,0:T(1,128)} %bitcast.3, ...), custom_call_target="tpu_custom_call" | custom-call | tf_op jit(solution)/shard_map/pallas_call | solution.py:346
  23.6 1.6 %copy.14 = bf16[1,64,1024]{2,1,0:T(8,128)(2,1)} copy(bf16[1,64,1024]{2,1,0:T(8,128)(2,1)} %shard_map.109) | data formatting | bytes 262144
